TPU v7x, 32 devices: a whole 2x2x4 slice. The times are simulated.
32 devices in a mesh: segment: 4 (over y, core), dp: 8 (over z, x).
Axes of the slice: x: 2, y: 2, z: 4, core: 2. Of those that a mesh axis runs over, the one named last changes fastest.
Arguments:
- token_ids: int32 [1024], P('dp'), may hold values from 0 to 38015, as said below
- table: bfloat16 [4752, 28672], P('segment', 'dp'), may hold values from -6 to 6
- out_grad: bfloat16 [1024, 3584], P('dp', 'segment'), may hold values from -6 to 6
Outputs:
- embedded: bfloat16 [1024, 3584], P('dp')
- table_grad: bfloat16 [4752, 28672], P('segment', 'dp')
Inputs may be any that keep to these rules, and one draw needn't show every extreme that they name: `token_ids`: in the 128 tokens of each data group, at most 16 ids lie in one segment's slice of 9504 rows with one residue modulo 8; in every data group some segment and residue has exactly 16.
All inputs are finite; a program needn't handle non-finite values.
Results may differ from a plain program's by a relative error of at most 0.001.
Values may be sent and summed in bfloat16 or wider, within the bound.
A program may use at most 64 MiB of HBM per device.

v0:
```python
import jax
import jax.numpy as jnp
from jax import lax
from jax.sharding import PartitionSpec as P

D = 3584
PACK = 8


def body(token_ids, table, out_grad):
    lines = table.shape[0]
    width = table.shape[1]
    groups = lax.axis_size("dp")
    tok_rows = token_ids.shape[0]
    quarters = D // width
    slot = lax.axis_index("dp") // quarters
    first = lax.axis_index("segment") * lines * PACK
    every_id = lax.all_gather(token_ids, "dp", axis=0, tiled=True)
    local = every_id - first
    in_section = (local >= 0) & (local < lines * PACK)
    owned = in_section & (local % PACK == slot)
    line_idx = jnp.clip(local // PACK, 0, lines - 1)
    whole_grad = lax.all_gather(out_grad, "segment", axis=1, tiled=True)
    capacity = tok_rows // PACK
    owned_grid = owned.reshape(groups, tok_rows)
    rank = jnp.cumsum(owned_grid.astype(jnp.int32), axis=1) - 1
    place = jnp.where(owned_grid, rank, capacity)
    group_rows = jnp.broadcast_to(jnp.arange(groups, dtype=jnp.int32)[:, None], (groups, tok_rows))
    row_of = (
        jnp.zeros((groups, capacity), jnp.int32)
        .at[group_rows, place]
        .set(line_idx.reshape(groups, tok_rows), mode="drop")
    )
    filled = jnp.zeros((groups, capacity), jnp.bool_).at[group_rows, place].set(True, mode="drop")
    fetched = jnp.take(table, row_of.reshape(-1), axis=0).reshape(groups, capacity, width)
    fetched = jnp.where(filled[:, :, None], fetched, jnp.zeros((), jnp.bfloat16))
    arrived = lax.all_to_all(fetched, "dp", split_axis=0, concat_axis=0, tiled=True)
    my_local = token_ids - first
    my_in = (my_local >= 0) & (my_local < lines * PACK)
    my_slot = my_local % PACK
    slot_hits = (my_slot[:, None] == jnp.arange(PACK, dtype=jnp.int32)[None, :]) & my_in[:, None]
    slot_ranks = jnp.cumsum(slot_hits.astype(jnp.int32), axis=0) - 1
    my_rank = jnp.sum(jnp.where(slot_hits, slot_ranks, 0), axis=1)
    sources = my_slot[:, None] * quarters + jnp.arange(quarters, dtype=jnp.int32)[None, :]
    flat_index = jnp.clip(sources * capacity + my_rank[:, None], 0, groups * capacity - 1)
    gathered = jnp.take(
        arrived.reshape(groups * capacity, width), flat_index.reshape(-1), axis=0
    ).reshape(tok_rows, D)
    segment_part = jnp.where(my_in[:, None], gathered.astype(jnp.float32), 0.0)
    slot_place = jnp.where(my_in, my_slot, PACK)
    token_at = (
        jnp.zeros((PACK, capacity), jnp.int32)
        .at[slot_place, my_rank]
        .set(jnp.arange(tok_rows, dtype=jnp.int32), mode="drop")
    )
    valid = jnp.zeros((PACK, capacity), jnp.bool_).at[slot_place, my_rank].set(True, mode="drop")
    grad_pick = jnp.take(whole_grad, token_at.reshape(-1), axis=0).reshape(
        PACK, capacity, quarters, width
    )
    grad_pick = jnp.where(valid[:, :, None, None], grad_pick, jnp.zeros((), jnp.bfloat16))
    grad_send = grad_pick.transpose(0, 2, 1, 3).reshape(groups, capacity, width)
    returned = lax.all_to_all(grad_send, "dp", split_axis=0, concat_axis=0, tiled=True)
    target = jnp.where(filled, row_of, lines)
    accum = (
        jnp.zeros((lines, width), jnp.float32)
        .at[target.reshape(-1)]
        .add(returned.reshape(-1, width).astype(jnp.float32), mode="drop")
    )
    embedded = lax.psum(segment_part.astype(jnp.bfloat16), "segment")
    return (embedded, accum.astype(jnp.bfloat16))


def solution(mesh):
    placed = (P("dp"), P("segment", "dp"), P("dp", "segment"))
    return jax.shard_map(
        body,
        mesh=mesh,
        in_specs=placed,
        out_specs=(P("dp", None), P("segment", "dp")),
        check_vma=False,
    )
```

profile of v0, /device:TPU:0, one launch (start us, length us, event | category | flops | bytes accessed | tf_op | source)
XLA Modules:
  0.0 159.1 jit_solution(7434590179938538914)
XLA Ops:
  7.2 22.6 %all-gather = s32[8,1,128]{2,1,0:T(1,128)S(1)} all-gather(s32[1,1,128]{2,1,0:T(1,128)} %bitcast.39), channel_id=1, replica_groups=mesh['segment'=4,'dp'=8] {'dp'}, dimensions={0}, use_global_device_ids=true | all-gather | bytes 4608 | tf_op jit(solution)/shard_map/all_gather | solution.py:18
  29.8 0.3 copy.12
  30.1 0.3 copy.13
  30.4 23.6 %compare_select_fusion = s32[8,128,1]{2,0,1:T(8,128)S(1)} fusion(pred[8,128,1]{2,0,1:T(8,128)(4,1)S(1)} %copy.13, s32[8,128,1]{2,0,1:T(8,128)S(1)} %copy.12), kind=kOutput, calls=%fused_computation.12 | output fusion | flops 135168 | bytes 9216 | tf_op jit(solution)/shard_map/jit(cumsum)/reduce_window_sum | solution.py:26
  54.0 0.2 copy.14
  54.2 0.8 multiply_reduce_fusion
  55.0 0.1 copy.19
  55.1 0.7 and_reduce_fusion
  55.8 0.1 copy.18
  56.0 4.3 %scatter_custom_fusion.4 = s32[128]{0:T(128)S(1)} fusion(s32[1024]{0:T(1024)S(1)} %bitcast.40, s32[1024]{0:T(1024)S(1)} %fusion.6, s32[]{:T(128)} %constant.70.clone.1), kind=kCustom, calls=%fused_computation.66 | custom fusion | bytes 516
  60.4 4.3 %scatter_custom_fusion.3 = pred[128]{0:T(512)(128)(4,1)S(1)} fusion(s32[1024]{0:T(1024)S(1)} %bitcast.41, pred[1024]{0:T(1024)(128)(4,1)S(1)} %broadcast.224, pred[]{:T(512)} %constant.71.clone.1), kind=kCustom, calls=%fused_computation.56 | custom fusion | bytes 129
  64.8 0.1 reshape.185
  64.9 6.6 %gather_fusion = bf16[128,3584]{1,0:T(8,128)(2,1)S(1)} fusion(bf16[1188,3584]{1,0:T(8,128)(2,1)} %param.6, s32[1024]{0:T(1024)S(1)} %pad_clamp_fusion.2), kind=kCustom, calls=%fused_computation.2 | custom fusion | bytes 1835520 | tf_op jit(solution)/shard_map/jit(_take)/gather | solution.py:35
  71.4 1.1 select_select_fusion
  72.6 3.6 %all-to-all-start = ((bf16[8,16,3584]{2,1,0:T(8,128)(2,1)}), bf16[8,16,3584]{2,1,0:T(8,128)(2,1)S(1)}, u32[]{:S(2)}, u32[]{:S(2)}) async-start(bf16[8,16,3584]{2,1,0:T(8,128)(2,1)} %select_select_fusion), calls=%async_computation | async-start | bytes 1835008 | tf_op jit(solution)/shard_map/all_to_all | solution.py:37
  76.2 0.1 fusion.4
  76.3 0.2 reduce_window_sum.23
  76.4 0.2 select_reduce_fusion
  76.7 6.4 %scatter_fusion.1 = s32[8,16]{1,0:T(8,128)S(1)} fusion(s32[8,16]{1,0:T(8,128)S(1)} %broadcast.169, s32[128]{0:T(128)S(1)} %fusion.18, s32[128]{0:T(128)S(1)} %iota.14), kind=kCustom, calls=%fused_computation.4 | custom fusion | bytes 2560 | tf_op jit(solution)/shard_map/scatter | solution.py:54
  83.0 0.1 reshape.180
  83.2 9.5 %all_gather.7 = bf16[128,3584]{1,0:T(8,128)(2,1)S(1)} all-gather(bf16[128,896]{1,0:T(8,128)(2,1)S(1)} %copy-done), channel_id=1, replica_groups=mesh['segment'=4,'dp'=8] {'segment'}, dimensions={1}, use_global_device_ids=true | all-gather | bytes 1146880 | tf_op jit(solution)/shard_map/all_gather | solution.py:23
  92.7 1.1 gather_fusion.2
  93.8 6.5 %scatter_fusion = pred[8,16]{1,0:T(8,128)(4,1)S(1)} fusion(pred[8,16]{1,0:T(8,128)(4,1)S(1)} %broadcast.166, s32[128]{0:T(128)S(1)} %fusion.18, pred[128]{0:T(512)(128)(4,1)S(1)} %broadcast.225), kind=kCustom, calls=%fused_computation.3 | custom fusion | bytes 1408 | tf_op jit(solution)/shard_map/scatter | solution.py:56
  100.3 0.2 broadcast_select_fusion
  100.5 1.1 broadcast_select_fusion.1
  101.5 5.9 %all-to-all-start.1 = ((bf16[8,16,3584]{2,1,0:T(8,128)(2,1)}), bf16[8,16,3584]{2,1,0:T(8,128)(2,1)S(1)}, u32[]{:S(2)}, u32[]{:S(2)}) async-start(bf16[8,16,3584]{2,1,0:T(8,128)(2,1)} %broadcast_select_fusion.1), calls=%async_computation.1 | async-start | bytes 1835008 | tf_op jit(solution)/shard_map/all_to_all | solution.py:62
  107.5 1.1 gather_fusion.1
  108.7 1.3 select_convert_fusion
  110.1 20.9 %all-to-all-done.1 = bf16[8,16,3584]{2,1,0:T(8,128)(2,1)S(1)} async-done(((bf16[8,16,3584]{2,1,0:T(8,128)(2,1)}), bf16[8,16,3584]{2,1,0:T(8,128)(2,1)S(1)}, u32[]{:S(2)}, u32[]{:S(2)}) %all-to-all-start.1) | async-done | bytes 917536 | tf_op jit(solution)/shard_map/all_to_all | solution.py:62
  130.9 10.0 %scatter_custom_fusion.2 = f32[1188,3584]{1,0:T(8,128)} fusion(s32[128]{0:T(128)S(1)} %fusion.16, f32[]{:T(128)} %constant.121.clone.1, bf16[128,3584]{1,0:T(8,128)(2,1)S(1)} %bitcast.35), kind=kCustom, calls=%fused_computation.8 | custom fusion | flops 917504 | bytes 17948676 | tf_op jit(solution)/shard_map/scatter-add | solution.py:67
  140.9 9.1 %convert_element_type.32 = bf16[1188,3584]{1,0:T(8,128)(2,1)} convert(f32[1188,3584]{1,0:T(8,128)} %scatter_custom_fusion.2) | non-fusion elementwise | flops 4257792 | bytes 25546752 | tf_op jit(solution)/shard_map/convert_element_type | solution.py:70
  150.1 2.2 %copy.23 = bf16[128,3584]{1,0:T(8,128)(2,1)} copy(bf16[128,3584]{1,0:T(8,128)(2,1)} %all-reduce.2.cloned.1.call-done) | data formatting | bytes 1835008
  (34 shorter events, 0.5 us)
Async XLA Ops:
  7.2 69.0 %copy-start.1 = (s32[128]{0:T(128)S(1)}, s32[128]{0:T(128)}, u32[]{:S(2)}) copy-start(s32[128]{0:T(128)} %param.5) | copy-start | bytes 1540
  7.2 76.0 %copy-start = (bf16[128,896]{1,0:T(8,128)(2,1)S(1)}, bf16[128,896]{1,0:T(8,128)(2,1)}, u32[]{:S(2)}) copy-start(bf16[128,896]{1,0:T(8,128)(2,1)} %param.7) | copy-start | bytes 688132
  72.6 29.0 %all-to-all-start = ((bf16[8,16,3584]{2,1,0:T(8,128)(2,1)}), bf16[8,16,3584]{2,1,0:T(8,128)(2,1)S(1)}, u32[]{:S(2)}, u32[]{:S(2)}) async-start(bf16[8,16,3584]{2,1,0:T(8,128)(2,1)} %select_select_fusion), calls=%async_computation | async-start | bytes 1835008 | tf_op jit(solution)/shard_map/all_to_all | solution.py:37
  101.5 29.4 %all-to-all-start.1 = ((bf16[8,16,3584]{2,1,0:T(8,128)(2,1)}), bf16[8,16,3584]{2,1,0:T(8,128)(2,1)S(1)}, u32[]{:S(2)}, u32[]{:S(2)}) async-start(bf16[8,16,3584]{2,1,0:T(8,128)(2,1)} %broadcast_select_fusion.1), calls=%async_computation.1 | async-start | bytes 1835008 | tf_op jit(solution)/shard_map/all_to_all | solution.py:62
  107.5 42.6 %all-reduce.2.cloned.1.call-start = ((), (), s32[]{:S(2)}) async-start(), calls=%async_computation.2 | async-start | bytes 1835008 | tf_op jit(solution)/shard_map/psum | solution.py:69
Sparse Core Ops, SparseCore 0:
  111.2 36.2 all-reduce.1
where the time goes:
time: 159 us
  other arithmetic  48.5 us (31%)
  local copies, waits for them, and re-layouts  33.8 us (21%)
  blocking collectives  32.1 us (20%)
  waiting for transfers between devices  20.9 us (13%)
  between operations  14.3 us (9%)
  starting transfers between devices  9.52 us (6%)
    another operation x1, other arithmetic, body(): rank = jnp.cumsum(owned_grid.astype(jnp.int32), axis=1) - 1  23.6 us
    all_gather x1, blocking collectives, body(): every_id = lax.all_gather(token_ids, 'dp', axis=0, tiled=True)  22.6 us
    all_to_all x1, waiting for transfers between devices, body(): lax.all_to_all(grad_send, 'dp', split_axis=0, concat_axis=0, tiled=True)  20.9 us
    unnamed x11, local copies, waits for them, and re-layouts  11.1 us
    scatter-add x1, other arithmetic, body(): accum = jnp.zeros((lines, width), jnp.float32).at[target.reshape(-1)].add...  10 us
    all_gather x1, blocking collectives, body(): whole_grad = lax.all_gather(out_grad, 'segment', axis=1, tiled=True)  9.52 us
    convert_element_type x1, other arithmetic, body(): return (embedded, accum.astype(jnp.bfloat16))  9.14 us
    gather x1, local copies, waits for them, and re-layouts, body(): jnp.take(table, row_of.reshape(-1), axis=0).reshape(groups, capacity, width)  6.55 us
  transfers between devices with their start and end apart: 3, of which 1 were waited for; matrix products, arithmetic and copies ran while one was open for 24% of the time, Pallas kernels for 0%

commit v1 on v0

--- a/solution.py
+++ b/solution.py
@@ -1,10 +1,23 @@
+import functools
 import jax
 import jax.numpy as jnp
 from jax import lax
 from jax.sharding import PartitionSpec as P
+from jax.lax import all_to_all, axis_size
 
 D = 3584
 PACK = 8
+
+
+def list_series(x_in, ax_name, axis_k):
+    prior = jnp.stack([x_in for _ in range(axis_size(ax_name))], axis=0)
+    field_out = jnp.concatenate(
+        all_to_all(prior, axis_name=ax_name, split_axis=0, concat_axis=0), axis=axis_k
+    )
+    return field_out
+
+
+lead_the_slabs = functools.partial(list_series, ax_name="dp", axis_k=0)
 
 
 def body(token_ids, table, out_grad):
@@ -15,7 +28,7 @@
     quarters = D // width
     slot = lax.axis_index("dp") // quarters
     first = lax.axis_index("segment") * lines * PACK
-    every_id = lax.all_gather(token_ids, "dp", axis=0, tiled=True)
+    every_id = lead_the_slabs(token_ids)
     local = every_id - first
     in_section = (local >= 0) & (local < lines * PACK)
     owned = in_section & (local % PACK == slot)

time: 159 us -> 145 us (0.912)
  other arithmetic: 48.5 us -> 25.9 us
  blocking collectives: 32.1 us -> 9.55 us
  waiting for transfers between devices: 20.9 us -> 42.8 us
  starting transfers between devices: 9.52 us -> 17 us
    another operation x1, other arithmetic: 23.6 us -> 0.45 us  [body(): rank = jnp.cumsum(owned_grid.astype(jnp.int32), axis=1) - 1]
    all_gather x1 -> x0, blocking collectives: 22.6 us -> none  [body(): every_id = lax.all_gather(token_ids, 'dp', axis=0, tiled=True)]
    all_to_all x1, waiting for transfers between devices: 0.01 us -> 22.2 us  [body(): lax.all_to_all(fetched, 'dp', split_axis=0, concat_axis=0, tiled=True)]
    all_to_all x0 -> x1, starting transfers between devices: none -> 7.28 us  [list_series(): all_to_all(prior, axis_name=ax_name, split_axis=0, concat_axis=0)]
    all_to_all x1, starting transfers between devices: 3.55 us -> 6 us  [body(): lax.all_to_all(fetched, 'dp', split_axis=0, concat_axis=0, tiled=True)]
    all_to_all x1, starting transfers between devices: 5.93 us -> 3.64 us  [body(): lax.all_to_all(grad_send, 'dp', split_axis=0, concat_axis=0, tiled=True)]
    unnamed x11 -> x10, local copies, waits for them, and re-layouts: 11.1 us -> 11 us
  transfers between devices with their start and end apart: 3 -> 4, of which waited for: 1 -> 2; matrix products, arithmetic and copies ran while one was open for 24% -> 27% of each run, Pallas kernels for 0% -> 0%
where the time goes in v1:
time: 145 us
  waiting for transfers between devices  42.8 us (30%)
  local copies, waits for them, and re-layouts  35.2 us (24%)
  other arithmetic  25.9 us (18%)
  starting transfers between devices  17 us (12%)
  between operations  14.3 us (10%)
  blocking collectives  9.55 us (7%)
    all_to_all x1, waiting for transfers between devices, body(): lax.all_to_all(fetched, 'dp', split_axis=0, concat_axis=0, tiled=True)  22.2 us
    all_to_all x1, waiting for transfers between devices, body(): lax.all_to_all(grad_send, 'dp', split_axis=0, concat_axis=0, tiled=True)  20.5 us
    unnamed x10, local copies, waits for them, and re-layouts  11 us
    scatter-add x1, other arithmetic, body(): accum = jnp.zeros((lines, width), jnp.float32).at[target.reshape(-1)].add...  10 us
    all_gather x1, blocking collectives, body(): whole_grad = lax.all_gather(out_grad, 'segment', axis=1, tiled=True)  9.55 us
    convert_element_type x1, other arithmetic, body(): return (embedded, accum.astype(jnp.bfloat16))  9.13 us
    all_to_all x1, starting transfers between devices, list_series(): all_to_all(prior, axis_name=ax_name, split_axis=0, concat_axis=0)  7.28 us
    gather x1, local copies, waits for them, and re-layouts, body(): jnp.take(table, row_of.reshape(-1), axis=0).reshape(groups, capacity, width)  6.56 us
  transfers between devices with their start and end apart: 4, of which 2 were waited for; matrix products, arithmetic and copies ran while one was open for 27% of the time, Pallas kernels for 0%

profile of v1, /device:TPU:0, one launch (start us, length us, event | category | flops | bytes accessed | tf_op | source)
XLA Modules:
  0.0 144.7 jit_solution(2342754970033430063)
XLA Ops:
  7.2 1.3 stack.2
  8.4 7.3 %all-to-all-start = ((s32[8,1,128]{2,1,0:T(1,128)}), s32[8,1,128]{2,1,0:T(1,128)S(1)}, u32[]{:S(2)}, u32[]{:S(2)}) async-start(s32[8,1,128]{2,1,0:T(1,128)} %stack.2), calls=%async_computation | async-start | bytes 8192 | tf_op jit(solution)/shard_map/all_to_all | solution.py:15
  15.7 0.7 compare_and_fusion.3
  16.4 0.7 and_select_fusion
  17.1 0.1 fusion.23
  17.2 0.2 reduce_window_sum.23
  17.3 0.2 select_reduce_fusion
  17.5 0.7 fusion.36
  18.2 6.4 %scatter_fusion.1 = s32[8,16]{1,0:T(8,128)S(1)} fusion(s32[8,16]{1,0:T(8,128)S(1)} %broadcast.283, s32[128]{0:T(128)S(1)} %fusion.36, s32[128]{0:T(128)S(1)} %iota.14), kind=kCustom, calls=%fused_computation.4 | custom fusion | bytes 2560 | tf_op jit(solution)/shard_map/scatter | solution.py:67
  24.7 9.6 %all_gather.3 = bf16[128,3584]{1,0:T(8,128)(2,1)S(1)} all-gather(bf16[128,896]{1,0:T(8,128)(2,1)} %param.7), channel_id=1, replica_groups=mesh['segment'=4,'dp'=8] {'segment'}, dimensions={1}, use_global_device_ids=true | all-gather | bytes 1146880 | tf_op jit(solution)/shard_map/all_gather | solution.py:36
  34.2 1.1 gather_fusion.2
  35.4 6.5 %scatter_fusion = pred[8,16]{1,0:T(8,128)(4,1)S(1)} fusion(pred[8,16]{1,0:T(8,128)(4,1)S(1)} %broadcast.281, s32[128]{0:T(128)S(1)} %fusion.36, pred[128]{0:T(512)(128)(4,1)S(1)} %broadcast.339), kind=kCustom, calls=%fused_computation.3 | custom fusion | bytes 1408 | tf_op jit(solution)/shard_map/scatter | solution.py:69
  41.9 0.3 copy.25
  42.2 0.5 broadcast_compare_fusion
  42.7 0.2 copy.32
  42.9 0.2 copy.31
  43.1 0.2 copy.30
  43.5 4.3 %scatter_custom_fusion.4 = s32[128]{0:T(128)S(1)} fusion(s32[1024]{0:T(1024)S(1)} %get-tuple-element.8, s32[1024]{0:T(1024)S(1)} %get-tuple-element.7, s32[]{:T(128)} %constant.108.clone.1), kind=kCustom, calls=%fused_computation.86 | custom fusion | bytes 516
  47.9 4.5 %scatter_custom_fusion.3 = pred[128]{0:T(512)(128)(4,1)S(1)} fusion(s32[1024]{0:T(1024)S(1)} %get-tuple-element.8, pred[1024]{0:T(1024)(128)(4,1)S(1)} %broadcast.338, pred[]{:T(512)} %constant.109.clone.1), kind=kCustom, calls=%fused_computation.76 | custom fusion | bytes 129
  52.6 6.6 %gather_fusion = bf16[128,3584]{1,0:T(8,128)(2,1)S(1)} fusion(bf16[1188,3584]{1,0:T(8,128)(2,1)} %param.6, s32[1024]{0:T(1024)S(1)} %pad_clamp_fusion.2), kind=kCustom, calls=%fused_computation.2 | custom fusion | bytes 1835520 | tf_op jit(solution)/shard_map/jit(_take)/gather | solution.py:48
  59.2 1.1 select_select_fusion
  60.3 6.0 %all-to-all-start.1 = ((bf16[8,16,3584]{2,1,0:T(8,128)(2,1)}), bf16[8,16,3584]{2,1,0:T(8,128)(2,1)S(1)}, u32[]{:S(2)}, u32[]{:S(2)}) async-start(bf16[8,16,3584]{2,1,0:T(8,128)(2,1)} %select_select_fusion), calls=%async_computation.1 | async-start | bytes 1835008 | tf_op jit(solution)/shard_map/all_to_all | solution.py:50
  66.3 0.1 broadcast_select_fusion
  66.4 1.1 broadcast_select_fusion.1
  67.5 22.2 %all-to-all-done.1 = bf16[8,16,3584]{2,1,0:T(8,128)(2,1)S(1)} async-done(((bf16[8,16,3584]{2,1,0:T(8,128)(2,1)}), bf16[8,16,3584]{2,1,0:T(8,128)(2,1)S(1)}, u32[]{:S(2)}, u32[]{:S(2)}) %all-to-all-start.1) | async-done | bytes 917536 | tf_op jit(solution)/shard_map/all_to_all | solution.py:50
  89.8 3.6 %all-to-all-start.2 = ((bf16[8,16,3584]{2,1,0:T(8,128)(2,1)}), bf16[8,16,3584]{2,1,0:T(8,128)(2,1)S(1)}, u32[]{:S(2)}, u32[]{:S(2)}) async-start(bf16[8,16,3584]{2,1,0:T(8,128)(2,1)} %broadcast_select_fusion.1), calls=%async_computation.2 | async-start | bytes 1835008 | tf_op jit(solution)/shard_map/all_to_all | solution.py:75
  93.5 1.1 gather_fusion.1
  94.6 1.3 select_convert_fusion
  96.0 20.5 %all-to-all-done.2 = bf16[8,16,3584]{2,1,0:T(8,128)(2,1)S(1)} async-done(((bf16[8,16,3584]{2,1,0:T(8,128)(2,1)}), bf16[8,16,3584]{2,1,0:T(8,128)(2,1)S(1)}, u32[]{:S(2)}, u32[]{:S(2)}) %all-to-all-start.2) | async-done | bytes 917536 | tf_op jit(solution)/shard_map/all_to_all | solution.py:75
  116.5 10.0 %scatter_custom_fusion.2 = f32[1188,3584]{1,0:T(8,128)} fusion(s32[128]{0:T(128)S(1)} %fusion.34, f32[]{:T(128)} %constant.123.clone.1, bf16[128,3584]{1,0:T(8,128)(2,1)S(1)} %bitcast.49), kind=kCustom, calls=%fused_computation.8 | custom fusion | flops 917504 | bytes 17948676 | tf_op jit(solution)/shard_map/scatter-add | solution.py:80
  126.6 9.1 %convert_element_type.32 = bf16[1188,3584]{1,0:T(8,128)(2,1)} convert(f32[1188,3584]{1,0:T(8,128)} %scatter_custom_fusion.2) | non-fusion elementwise | flops 4257792 | bytes 25546752 | tf_op jit(solution)/shard_map/convert_element_type | solution.py:83
  135.7 2.2 %copy.42 = bf16[128,3584]{1,0:T(8,128)(2,1)} copy(bf16[128,3584]{1,0:T(8,128)(2,1)} %all-reduce.2.cloned.1.call-done) | data formatting | bytes 1835008
  (36 shorter events, 0.7 us)
Async XLA Ops:
  7.2 36.2 %copy-start.2 = (s32[2]{0:T(128)S(1)}, s32[2]{0:T(128)}, u32[]{:S(2)}) copy-start(s32[2]{0:T(128)} %constant.124) | copy-start | bytes 28
  7.2 36.3 %copy-start.1 = (s32[2]{0:T(128)S(1)}, s32[2]{0:T(128)}, u32[]{:S(2)}) copy-start(s32[2]{0:T(128)} %constant.127) | copy-start | bytes 28
  8.4 33.4 %all-to-all-start = ((s32[8,1,128]{2,1,0:T(1,128)}), s32[8,1,128]{2,1,0:T(1,128)S(1)}, u32[]{:S(2)}, u32[]{:S(2)}) async-start(s32[8,1,128]{2,1,0:T(1,128)} %stack.2), calls=%async_computation | async-start | bytes 8192 | tf_op jit(solution)/shard_map/all_to_all | solution.py:15
  52.6 40.9 %copy-start = (s32[128]{0:T(128)S(1)}, s32[128]{0:T(128)}, u32[]{:S(2)}) copy-start(s32[128]{0:T(128)} %param.5) | copy-start | bytes 1540
  60.3 29.5 %all-to-all-start.1 = ((bf16[8,16,3584]{2,1,0:T(8,128)(2,1)}), bf16[8,16,3584]{2,1,0:T(8,128)(2,1)S(1)}, u32[]{:S(2)}, u32[]{:S(2)}) async-start(bf16[8,16,3584]{2,1,0:T(8,128)(2,1)} %select_select_fusion), calls=%async_computation.1 | async-start | bytes 1835008 | tf_op jit(solution)/shard_map/all_to_all | solution.py:50
  89.8 26.8 %all-to-all-start.2 = ((bf16[8,16,3584]{2,1,0:T(8,128)(2,1)}), bf16[8,16,3584]{2,1,0:T(8,128)(2,1)S(1)}, u32[]{:S(2)}, u32[]{:S(2)}) async-start(bf16[8,16,3584]{2,1,0:T(8,128)(2,1)} %broadcast_select_fusion.1), calls=%async_computation.2 | async-start | bytes 1835008 | tf_op jit(solution)/shard_map/all_to_all | solution.py:75
  93.4 42.3 %all-reduce.2.cloned.1.call-start = ((), (), s32[]{:S(2)}) async-start(), calls=%async_computation.3 | async-start | bytes 1835008 | tf_op jit(solution)/shard_map/psum | solution.py:82
Sparse Core Ops, SparseCore 0:
  97.2 36.1 all-reduce.1
